TPU v7x, 256 devices: a whole 4x4x8 slice. The times are simulated.
256 devices in a mesh: bank: 16 (over y, x), zero: 16 (over z, core).
Axes of the slice: x: 4, y: 4, z: 8, core: 2. Of those that a mesh axis runs over, the one named last changes fastest.
Arguments:
- w_down: float32 [64, 1024, 2048], P('bank', None, 'zero'), may hold values from -0.25 to 0.25
- avg_down: bfloat16 [64, 1024, 2048], P('bank', None, 'zero'), may hold values from -0.09375 to 0.09375
- router_weight: float32 [2048, 64], P('zero', 'bank'), may hold values from -0.125 to 0.125
- router_gain: float32 [2048], P('zero'), may hold values from 0.25 to 1.75
Outputs:
- serve_down: bfloat16 [64, 1024, 2048], P('bank')
- scale_down: float32 [64, 1024], P('bank')
- serve_router: bfloat16 [2048, 64], replicated
All inputs are finite; a program needn't handle non-finite values.
Results may differ from a plain program's by a relative error of at most 0.001.
Values may be sent and summed in bfloat16 or wider, within the bound.
A program may use at most 128 MiB of HBM per device.

v0:
```python
import jax
import jax.numpy as jnp
from jax import lax
from jax.sharding import PartitionSpec as P


def copy_for_each(x, axis):
    copies = jnp.broadcast_to(x, (lax.axis_size(axis), *x.shape))
    return lax.all_to_all(copies, axis, split_axis=0, concat_axis=0, tiled=True)


def over_copies(x, axis):
    return copy_for_each(x, axis).sum(axis=0)


def in_order(parts, dim):
    dims = list(parts.shape[1:])
    dims[dim] *= parts.shape[0]
    return jnp.moveaxis(parts, 0, dim).reshape(dims)


def gather_directly(x, axis, dim):
    parts = copy_for_each(x, axis)
    return in_order(parts, dim)


def shards(w_down, avg_down, router_weight, router_gain):
    fresh_down = w_down + avg_down.astype(jnp.float32)
    total_down = over_copies(jnp.sum(fresh_down * fresh_down, axis=2), "zero")
    scale_down = jnp.sqrt(total_down)
    narrow_down = (fresh_down / jnp.expand_dims(scale_down, 2)).astype(jnp.bfloat16)
    serve_down = lax.all_gather(narrow_down, "zero", axis=2, tiled=True)
    part_router = (router_weight * router_gain[:, None]).astype(jnp.bfloat16)
    row_router = gather_directly(part_router, "zero", 0)
    serve_router = gather_directly(row_router, "bank", 1)
    return (serve_down, scale_down, serve_router)


def solution(mesh):
    return jax.shard_map(
        shards,
        mesh=mesh,
        in_specs=(P("bank", None, "zero"), P("bank", None, "zero"), P("zero", "bank"), P("zero")),
        out_specs=(P("bank", None, None), P("bank", None), P()),
        check_vma=False,
    )
```

profile of v0, /device:TPU:1, one launch (start us, length us, event | category | flops | bytes accessed | tf_op | source)
XLA Modules:
  0.0 152.9 jit_solution(14177765800500866044)
XLA Ops:
  7.2 0.0 copy-start
  7.2 0.0 copy-start.1
  7.2 0.0 all-gather.2.cloned.1.call-start
  7.2 2.6 %multiply_reduce_fusion = f32[4,1024]{1,0:T(4,128)S(1)} fusion(f32[4,1024,128]{2,1,0:T(8,128)} %param.4, bf16[4,1024,128]{2,1,0:T(8,128)(2,1)} %param.5), kind=kLoop, calls=%fused_computation.1 | loop fusion | flops 2093056 | bytes 3162112 | tf_op jit(solution)/shard_map/reduce_sum | solution.py:29
  9.9 21.4 %all_to_all.15 = f32[16,4,1024]{2,1,0:T(4,128)S(1)} all-to-all(f32[16,4,1024]{2,1,0:T(4,128)S(1)} %broadcast_in_dim.11), channel_id=1, replica_groups=mesh['bank'=16,'zero'=16] {'zero'}, dimensions={0} | all-to-all | bytes 524288 | tf_op jit(solution)/shard_map/all_to_all | solution.py:9
  31.3 0.1 reduce_sum.19
  31.3 0.0 copy-done
  31.4 0.0 copy-done.1
  31.4 0.0 copy-start.2
  31.4 0.0 copy-start.3
  31.4 0.0 copy-start.4
  31.4 1.5 divide_convert_fusion
  32.9 0.0 copy-done.2
  32.9 0.0 all-gather.2.cloned.1.call-update
  32.9 0.0 copy-done.3
  33.0 0.0 copy-done.4
  33.0 10.1 %all_to_all.16 = bf16[16,128,4]{1,2,0:T(4,128)(2,1)S(1)} all-to-all(bf16[16,128,4]{1,2,0:T(4,128)(2,1)S(1)} %broadcast_in_dim.12), channel_id=1, replica_groups=mesh['bank'=16,'zero'=16] {'zero'}, dimensions={0} | all-to-all | bytes 32768 | tf_op jit(solution)/shard_map/all_to_all | solution.py:9
  43.1 0.1 broadcast_in_dim.13
  43.2 14.7 %all_to_all.17 = bf16[16,2048,4]{1,2,0:T(4,128)(2,1)S(1)} all-to-all(bf16[16,2048,4]{1,2,0:T(4,128)(2,1)S(1)} %broadcast_in_dim.13), channel_id=1, replica_groups=mesh['bank'=16,'zero'=16] {'bank'}, dimensions={0} | all-to-all | bytes 524288 | tf_op jit(solution)/shard_map/all_to_all | solution.py:9
  57.9 0.8 reshape.17
  58.6 73.3 %all-gather.2.cloned.1.call-done = bf16[4,1024,2048]{2,1,0:T(8,128)(2,1)} async-done(((bf16[4,1024,128]{2,1,0:T(8,128)(2,1)}), bf16[4,1024,2048]{2,1,0:T(8,128)(2,1)}) %all-gather.2.cloned.1.call-update) | async-done | bytes 16777232 | tf_op jit(solution)/shard_map/all_gather | solution.py:32
  131.9 14.2 %copy.10 = bf16[4,1024,2048]{2,1,0:T(8,128)(2,1)} copy(bf16[4,1024,2048]{2,1,0:T(8,128)(2,1)} %all-gather.2.cloned.1.call-done) | data formatting | bytes 33554432
  (4 shorter events, 0.1 us)
Async XLA Ops:
  7.2 24.2 %copy-start = (f32[4,1024,128]{2,1,0:T(8,128)S(1)}, f32[4,1024,128]{2,1,0:T(8,128)}, u32[]{:S(2)}) copy-start(f32[4,1024,128]{2,1,0:T(8,128)} %param.4) | copy-start | bytes 6291460
  7.2 24.2 %copy-start.1 = (bf16[4,1024,128]{2,1,0:T(8,128)(2,1)S(1)}, bf16[4,1024,128]{2,1,0:T(8,128)(2,1)}, u32[]{:S(2)}) copy-start(bf16[4,1024,128]{2,1,0:T(8,128)(2,1)} %param.5) | copy-start | bytes 3145732
  7.2 124.7 %all-gather.2.cloned.1.call-start = ((), (), s32[]{:S(2)}) async-start(), calls=%async_computation.3 | async-start | bytes 17825792 | tf_op jit(solution)/shard_map/all_gather | solution.py:32
  31.4 1.6 %copy-start.2 = (f32[4,1024]{1,0:T(4,128)}, f32[4,1024]{1,0:T(4,128)S(1)}, u32[]{:S(2)}) copy-start(f32[4,1024]{1,0:T(4,128)S(1)} %sqrt.7) | copy-start | bytes 49156
  31.4 1.6 %copy-start.3 = (f32[128,4]{0,1:T(4,128)S(1)}, f32[128,4]{0,1:T(4,128)}, u32[]{:S(2)}) copy-start(f32[128,4]{0,1:T(4,128)} %param.6) | copy-start | bytes 6148
  31.4 1.6 %copy-start.4 = (f32[128]{0:T(128)S(1)}, f32[128]{0:T(128)}, u32[]{:S(2)}) copy-start(f32[128]{0:T(128)} %param.7) | copy-start | bytes 1540
Sparse Core Ops, SparseCore 0:
  33.1 98.8 all-gather.1
where the time goes:
time: 153 us
  waiting for transfers between devices  73.3 us (48%)
  blocking collectives  46.1 us (30%)
  local copies, waits for them, and re-layouts  15.1 us (10%)
  between operations  14.1 us (9%)
  other arithmetic  4.21 us (3%)
    all_gather x1, waiting for transfers between devices, shards(): serve_down = lax.all_gather(narrow_down, 'zero', axis=2, tiled=True)  73.3 us
    all_to_all x3, blocking collectives, copy_for_each(): return lax.all_to_all(copies, axis, split_axis=0, concat_axis=0, tiled=True)  46.1 us
    unnamed x11, local copies, waits for them, and re-layouts  14.2 us
  transfers between devices with their start and end apart: 1, of which 1 were waited for; matrix products, arithmetic and copies ran while one was open for 1% of the time, Pallas kernels for 0%

commit v1 on v0

v1 whole, which is shorter than its diff:
```python
import functools

import jax
import jax.numpy as jnp
from jax import lax
from jax.experimental import pallas as pl
from jax.experimental.pallas import tpu as pltpu
from jax.sharding import PartitionSpec as P

MESH = pl.DeviceIdType.MESH
SPLIT = 2


def gather_kernel(
    banks, chips, w_hbm, avg_hbm, rw_hbm, gain_hbm,
    big, scale_ref, router_ref,
    wbuf, abuf, rw_ref, gain_ref, part, other, sums, total, rblk,
    wsem, asem, osem, ssem, tsem,
    rsem_r, rsem_l, send_r, send_l, send_p, recv_p, misc_send, rz_recv, rb_recv, rp_recv,
):
    experts, rows, lanes = wbuf.shape
    bank = lax.axis_index("bank")
    zero = lax.axis_index("zero")
    z = zero // 2
    core = zero % 2
    right = ((z + 1) % chips) * 2 + core
    left = ((z + chips - 1) % chips) * 2 + core
    partner = z * 2 + (1 - core)
    half = experts // 2
    groups = rows // lanes
    piece = rows // SPLIT
    chunks = experts * SPLIT
    reach = chips // 2

    small = [pltpu.make_async_copy(rw_hbm, rw_ref, asem.at[experts]),
             pltpu.make_async_copy(gain_hbm, gain_ref, wsem.at[experts])]
    loads = []
    for e in range(experts):
        lw = pltpu.make_async_copy(w_hbm.at[e], wbuf.at[e], wsem.at[e])
        la = pltpu.make_async_copy(avg_hbm.at[e], abuf.at[e], asem.at[e])
        lw.start()
        la.start()
        loads.append((lw, la))
    for copy in small:
        copy.start()

    barrier = pltpu.get_barrier_semaphore()
    pl.semaphore_signal(barrier, inc=1, device_id={"zero": partner}, device_id_type=MESH)
    for j in range(1, chips):
        peer = ((z + j) % chips) * 2 + core
        pl.semaphore_signal(barrier, inc=1, device_id={"zero": peer}, device_id_type=MESH)
    for j in range(1, banks):
        peer = (bank + j) % banks
        pl.semaphore_signal(barrier, inc=1, device_id={"bank": peer}, device_id_type=MESH)

    eye = (
        lax.broadcasted_iota(jnp.int32, (lanes, lanes), 0)
        == lax.broadcasted_iota(jnp.int32, (lanes, lanes), 1)
    )
    for e in range(experts):
        loads[e][0].wait()
        loads[e][1].wait()
        for g in range(groups):
            at = pl.ds(g * lanes, lanes)
            fresh = wbuf[e, at, :] + abuf[e, at, :].astype(jnp.float32)
            wbuf[e, at, :] = fresh
            row = jnp.sum(fresh * fresh, axis=1, keepdims=True)
            part[e, g:g + 1, :] = jnp.sum(jnp.where(eye, row, 0.0), axis=0, keepdims=True)

    for copy in small:
        copy.wait()
    rblk[bank, zero] = rw_ref[...] * gain_ref[...]

    pl.semaphore_wait(barrier, 1 + (chips - 1) + (banks - 1))

    mine, theirs = pl.ds(core * half, half), pl.ds((1 - core) * half, half)
    swap = pltpu.make_async_remote_copy(
        part.at[theirs], other, osem.at[0], osem.at[1],
        device_id={"zero": partner}, device_id_type=MESH)
    swap.start()
    rz = []
    for j in range(1, chips):
        peer = ((z + j) % chips) * 2 + core
        rz.append(pltpu.make_async_remote_copy(
            rblk.at[bank, zero], rblk.at[bank, zero], misc_send.at[0], rz_recv,
            device_id={"zero": peer}, device_id_type=MESH))
    swap.wait()
    sums[z] = part[mine] + other[...]
    spread = []
    for j in range(1, chips):
        peer = ((z + j) % chips) * 2 + core
        spread.append(pltpu.make_async_remote_copy(
            sums.at[z], sums.at[z], ssem.at[0], ssem.at[1],
            device_id={"zero": peer}, device_id_type=MESH))
    for copy in spread:
        copy.start()
    for copy in rz:
        copy.start()
    full = pltpu.make_async_remote_copy(
        sums.at[pl.ds(0, chips - 1)], sums.at[pl.ds(0, chips - 1)], ssem.at[0], ssem.at[1],
        device_id={"zero": partner}, device_id_type=MESH)
    full.wait_recv()
    acc = sums[0]
    for k in range(1, chips):
        acc = acc + sums[k]
    total[mine] = acc
    back = pltpu.make_async_remote_copy(
        total.at[mine], total.at[mine], tsem.at[0], tsem.at[1],
        device_id={"zero": partner}, device_id_type=MESH)
    back.start()
    back.wait_recv()

    def place(k, src):
        return big.at[k // SPLIT, pl.ds((k % SPLIT) * piece, piece),
                      pl.ds(pl.multiple_of(src * lanes, lanes), lanes)]

    def to_right(slot, k, src):
        return pltpu.make_async_remote_copy(
            place(k, src), place(k, src), send_r, rsem_r.at[slot],
            device_id={"zero": right}, device_id_type=MESH)

    def to_left(slot, k, src):
        return pltpu.make_async_remote_copy(
            place(k, src), place(k, src), send_l, rsem_l.at[slot],
            device_id={"zero": left}, device_id_type=MESH)

    def to_partner(k, src):
        return pltpu.make_async_remote_copy(
            place(k, src), place(k, src), send_p, recv_p,
            device_id={"zero": partner}, device_id_type=MESH)

    columns = pl.ds(pl.multiple_of(zero * lanes, lanes), lanes)
    for e in range(experts):
        root = jnp.sqrt(total[e])
        for g in range(groups):
            scale_ref[e:e + 1, g * lanes:(g + 1) * lanes] = root[g:g + 1, :]
        for s in range(SPLIT):
            for g in range(s * groups // SPLIT, (s + 1) * groups // SPLIT):
                at = pl.ds(g * lanes, lanes)
                col = jnp.sum(jnp.where(eye, root[g:g + 1, :], 0.0), axis=1, keepdims=True)
                big[e, at, columns] = (wbuf[e, at, :] / col).astype(jnp.bfloat16)
            k = e * SPLIT + s
            to_right(k, k, zero).start()
            to_left(k, k, zero).start()
            to_partner(k, zero).start()

    def router_banks():
        pltpu.make_async_remote_copy(
            rblk.at[bank, pl.ds(0, chips - 1)], rblk.at[bank, pl.ds(0, chips - 1)], misc_send.at[0], rz_recv,
            device_id={"zero": partner}, device_id_type=MESH).wait()
        for j in range(1, banks):
            peer = (bank + j) % banks
            for q in range(chips):
                pltpu.make_async_remote_copy(
                    rblk.at[bank, 2 * q + core], rblk.at[bank, 2 * q + core], misc_send.at[1], rb_recv,
                    device_id={"bank": peer}, device_id_type=MESH).start()

    def router_partner():
        n = (banks - 1) * chips
        def all_of(ref):
            return ref.at[pl.ds(0, banks - 1), pl.ds(0, chips)]
        pltpu.make_async_remote_copy(
            all_of(rblk), all_of(rblk), misc_send.at[1], rb_recv,
            device_id={"zero": partner}, device_id_type=MESH).wait()
        for q in range(chips):
            pltpu.make_async_remote_copy(
                rblk.at[:, 2 * q + core], rblk.at[:, 2 * q + core], misc_send.at[2], rp_recv,
                device_id={"zero": partner}, device_id_type=MESH).start()

    def router_finish():
        def all_of(ref):
            return ref.at[:, pl.ds(0, chips)]
        pltpu.make_async_remote_copy(
            all_of(rblk), all_of(rblk), misc_send.at[2], rp_recv,
            device_id={"zero": partner}, device_id_type=MESH).wait()
        for b in range(banks // 4):
            for q in range(2 * chips):
                block = jnp.concatenate([rblk[4 * b + i, q] for i in range(4)], axis=0)
                n = block.shape[0]
                router_ref[b * n:(b + 1) * n, q * lanes:(q + 1) * lanes] = block.astype(jnp.bfloat16)

    slot = 0
    for d in range(1, reach + 1):
        from_left = ((z + chips - d) % chips) * 2 + core
        from_right = ((z + d) % chips) * 2 + core
        last = d == reach
        for i in range(chunks // 2 if last else chunks):
            kr = 2 * i if last else i
            kl = 2 * i + 1 if last else i
            to_right(slot, kr, from_left).wait_recv()
            if d + 1 < reach:
                to_right(slot + chunks, kr, from_left).start()
            elif d + 1 == reach and kr % 2 == 0:
                to_right(d * chunks + kr // 2, kr, from_left).start()
            to_partner(kr, from_left).start()
            to_left(slot, kl, from_right).wait_recv()
            if d + 1 < reach:
                to_left(slot + chunks, kl, from_right).start()
            elif d + 1 == reach and kl % 2 == 1:
                to_left(d * chunks + kl // 2, kl, from_right).start()
            to_partner(kl, from_right).start()
            slot += 1
        if d == 1:
            router_banks()
        if d == min(2, reach):
            router_partner()
        if d == min(3, reach):
            router_finish()

    side = pl.ds(0, chips)
    def cols(n):
        return big.at[:, :, pl.ds(0, n * lanes)]
    def wide(n):
        return big.at[pl.ds(0, experts // 2), :, pl.ds(0, n * lanes)]
    hops = wide(chips - 1)
    whole = cols(chips)
    swap_back = back
    swap_back.wait_send()
    full.wait_send()
    pltpu.make_async_remote_copy(hops, hops, send_r, rsem_r.at[0],
                                 device_id={"zero": right}, device_id_type=MESH).wait_send()
    pltpu.make_async_remote_copy(hops, hops, send_l, rsem_l.at[0],
                                 device_id={"zero": left}, device_id_type=MESH).wait_send()
    pltpu.make_async_remote_copy(whole, whole, send_p, recv_p,
                                 device_id={"zero": partner}, device_id_type=MESH).wait()


def out_kernel(big, scale, router, big_hbm, scale_hbm, router_hbm, sems):
    n = big.shape[0]
    copies = [pltpu.make_async_copy(big.at[e], big_hbm.at[e], sems.at[e]) for e in range(n)]
    copies.append(pltpu.make_async_copy(scale, scale_hbm, sems.at[n]))
    copies.append(pltpu.make_async_copy(router, router_hbm, sems.at[n + 1]))
    for copy in copies:
        copy.start()
    for copy in copies:
        copy.wait()


def solution(mesh):
    banks, zeros = mesh.shape["bank"], mesh.shape["zero"]
    chips = zeros // 2

    def shards(w_down, avg_down, router_weight, router_gain):
        experts, rows, lanes = w_down.shape
        width = lanes * zeros
        cols = router_weight.shape[1]
        vmem = pl.BlockSpec(memory_space=pltpu.VMEM)
        hbm = pl.BlockSpec(memory_space=pltpu.HBM)
        pin = lambda x: pltpu.with_memory_space_constraint(x, pltpu.HBM)
        half = experts // 2
        groups = rows // lanes
        slots = experts * SPLIT * (chips - 1) // 2
        dma = pltpu.SemaphoreType.DMA
        big, scale, router = pl.pallas_call(
            functools.partial(gather_kernel, banks, chips),
            out_shape=(
                jax.ShapeDtypeStruct((experts, rows, width), jnp.bfloat16),
                jax.ShapeDtypeStruct((experts, rows), jnp.float32),
                jax.ShapeDtypeStruct((cols * banks, width), jnp.bfloat16),
            ),
            in_specs=[hbm] * 4,
            out_specs=(vmem, vmem, vmem),
            scratch_shapes=[
                pltpu.VMEM((experts, rows, lanes), jnp.float32),
                pltpu.VMEM((experts, rows, lanes), jnp.bfloat16),
                pltpu.VMEM((cols, lanes), jnp.float32),
                pltpu.VMEM((1, lanes), jnp.float32),
                pltpu.VMEM((experts, groups, lanes), jnp.float32),
                pltpu.VMEM((half, groups, lanes), jnp.float32),
                pltpu.VMEM((chips, half, groups, lanes), jnp.float32),
                pltpu.VMEM((experts, groups, lanes), jnp.float32),
                pltpu.VMEM((banks, zeros, cols, lanes), jnp.float32),
                dma((experts + 1,)), dma((experts + 1,)), dma((2,)), dma((2,)), dma((2,)),
                dma((slots,)), dma((slots,)), dma(()), dma(()), dma(()), dma(()),
                dma((3,)), dma(()), dma(()), dma(()),
            ],
            compiler_params=pltpu.CompilerParams(
                collective_id=0, has_side_effects=True, vmem_limit_bytes=8 * 1024 * 1024),
            name="gather",
        )(pin(w_down), pin(avg_down), pin(router_weight.T), pin(router_gain.reshape(1, lanes)))
        big, scale, router = pl.pallas_call(
            out_kernel,
            out_shape=(
                jax.ShapeDtypeStruct(big.shape, big.dtype),
                jax.ShapeDtypeStruct(scale.shape, scale.dtype),
                jax.ShapeDtypeStruct(router.shape, router.dtype),
            ),
            in_specs=[vmem, vmem, vmem],
            out_specs=(hbm, hbm, hbm),
            scratch_shapes=[dma((experts + 2,))],
            compiler_params=pltpu.CompilerParams(vmem_limit_bytes=4 * 1024 * 1024),
            name="put_out",
        )(big, scale, router)
        return big, scale, router.T

    return jax.shard_map(
        shards,
        mesh=mesh,
        in_specs=(P("bank", None, "zero"), P("bank", None, "zero"), P("zero", "bank"), P("zero")),
        out_specs=(P("bank", None, None), P("bank", None), P()),
        check_vma=False,
    )
```

time: 153 us -> 107 us (0.70)
  Pallas kernels: 0 us -> 106 us
  waiting for transfers between devices: 73.3 us -> 0 us
  blocking collectives: 46.1 us -> 0 us
  local copies, waits for them, and re-layouts: 15.1 us -> 0 us
  between operations: 14.1 us -> 0.64 us
  other arithmetic: 4.21 us -> 0 us
    pallas_call x0 -> x2, Pallas kernels: none -> 106 us  [the longest x1 100 us: shards(): pl.pallas_call(functools.partial(gather_kernel, banks, chips), out_shape=...]
    all_gather x1 -> x0, waiting for transfers between devices: 73.3 us -> none  [shards(): serve_down = lax.all_gather(narrow_down, 'zero', axis=2, tiled=True)]
    all_to_all x3 -> x0, blocking collectives: 46.1 us -> none  [copy_for_each(): return lax.all_to_all(copies, axis, split_axis=0, concat_axis=0, tiled=True)]
    unnamed x11 -> x0, local copies, waits for them, and re-layouts: 14.2 us -> none
    reduce_sum x2 -> x0, other arithmetic: 2.68 us -> none  [the longest x1 2.63 us: shards(): total_down = over_copies(jnp.sum(fresh_down * fresh_down, axis=2), 'zero')]
  transfers between devices with their start and end apart: 1 -> 0, of which waited for: 1 -> 0; matrix products, arithmetic and copies ran while one was open for 1% -> 0% of each run, Pallas kernels for 0% -> 0%
where the time goes in v1:
time: 107 us
  Pallas kernels  106 us (99%)
    pallas_call x1, Pallas kernels, shards(): pl.pallas_call(functools.partial(gather_kernel, banks, chips), out_shape=...  100 us
    pallas_call x1, Pallas kernels, shards(): pl.pallas_call(out_kernel, out_shape=(jax.ShapeDtypeStruct(big.shape, big...  5.98 us

profile of v1, /device:TPU:1, one launch (start us, length us, event | category | flops | bytes accessed | tf_op | source)
XLA Modules:
  0.0 106.8 jit_solution(15026650719341453405)
XLA Ops:
  0.6 100.2 %gather.1 = (bf16[4,1024,2048]{2,1,0:T(8,128)(2,1)S(1)}, f32[4,1024]{1,0:T(4,128)S(1)}, bf16[64,2048]{1,0:T(8,128)(2,1)S(1)}) custom-call(f32[4,1024,128]{2,1,0:T(8,128)} %w_hbm.1, bf16[4,1024,128]{2,1,0:T(8,128)(2,1)} %avg_hbm.1, f32[4,128]{1,0:T(4,128)} %bitcast.3, f32[1,128]{1,0:T(1,128)} %bitcast.4), custom_call_target="tpu_custom_call" | custom-call | tf_op jit(solution)/shard_map/gather/pallas_call | solution.py:254
  100.8 6.0 %put_out.1 = (bf16[4,1024,2048]{2,1,0:T(8,128)(2,1)}, f32[4,1024]{1,0:T(4,128)}, bf16[64,2048]{1,0:T(8,128)(2,1)}) custom-call(bf16[4,1024,2048]{2,1,0:T(8,128)(2,1)S(1)} %get-tuple-element.9.big, f32[4,1024]{1,0:T(4,128)S(1)} %get-tuple-element.10.scale, bf16[64,2048]{1,0:T(8,128)(2,1)S(1)} %get-tuple-element.11.router), custom_call_target="tpu_custom_call" | custom-call | tf_op jit(solution)/shard_map/put_out/pallas_call | solution.py:281

commit v2 on v1

v2 whole, which is shorter than its diff:
```python
import functools

import jax
import jax.numpy as jnp
from jax import lax
from jax.experimental import pallas as pl
from jax.experimental.pallas import tpu as pltpu
from jax.sharding import PartitionSpec as P

MESH = pl.DeviceIdType.MESH
SPLIT = 4
EARLY = 3
FIRST = 128
SIDE = 4


def gather_kernel(
    banks, chips, w_hbm, avg_hbm, rw_hbm, gain_hbm,
    big, scale_ref, router_ref,
    wbuf, abuf, rw_ref, gain_ref, part, other, sums, total, rblk, from_l, from_r,
    wsem, asem, osem, ssem, tsem, tok_l, tok_r,
    rsem_r, rsem_l, send_r, send_l, esend_r, esend_l, erecv_r, erecv_l, send_p, recv_p, rsend, rrecv,
):
    experts, rows, lanes = wbuf.shape
    bank = lax.axis_index("bank")
    zero = lax.axis_index("zero")
    z = zero // 2
    core = zero % 2
    y, x = bank // SIDE, bank % SIDE
    tall = banks // SIDE
    right = {"zero": ((z + 1) % chips) * 2 + core}
    left = {"zero": ((z + chips - 1) % chips) * 2 + core}
    partner = {"zero": z * 2 + (1 - core)}
    x_up, x_down = {"bank": y * SIDE + (x + 1) % SIDE}, {"bank": y * SIDE + (x + SIDE - 1) % SIDE}
    y_up, y_down = {"bank": ((y + 1) % tall) * SIDE + x}, {"bank": ((y + tall - 1) % tall) * SIDE + x}
    half = experts // 2
    groups = rows // lanes
    piece = rows // SPLIT
    chunks = experts * SPLIT
    reach = chips // 2
    ahead = EARLY * piece

    def remote(src, dst, send, recv, to):
        return pltpu.make_async_remote_copy(src, dst, send, recv, device_id=to, device_id_type=MESH)

    def signal(sem, to):
        pl.semaphore_signal(sem, inc=1, device_id=to, device_id_type=MESH)

    small = [pltpu.make_async_copy(rw_hbm, rw_ref, asem.at[experts]),
             pltpu.make_async_copy(gain_hbm, gain_ref, wsem.at[experts])]
    loads = []
    for e in range(experts):
        lw = pltpu.make_async_copy(w_hbm.at[e], wbuf.at[e], wsem.at[e])
        la = pltpu.make_async_copy(avg_hbm.at[e], abuf.at[e], asem.at[e])
        lw.start()
        la.start()
        loads.append((lw, la))
    for copy in small:
        copy.start()

    barrier = pltpu.get_barrier_semaphore()
    near = (left, right, partner, x_up, x_down, y_up, y_down)
    for to in near:
        signal(barrier, to)

    eye = (
        lax.broadcasted_iota(jnp.int32, (lanes, lanes), 0)
        == lax.broadcasted_iota(jnp.int32, (lanes, lanes), 1)
    )

    def square(e):
        loads[e][0].wait()
        loads[e][1].wait()
        for g in range(groups):
            at = pl.ds(g * lanes, lanes)
            fresh = wbuf[e, at, :] + abuf[e, at, :].astype(jnp.float32)
            wbuf[e, at, :] = fresh
            row = jnp.sum(fresh * fresh, axis=1, keepdims=True)
            part[e, g:g + 1, :] = jnp.sum(jnp.where(eye, row, 0.0), axis=0, keepdims=True)

    def early(at):
        remote(wbuf.at[0, at], from_l.at[at], esend_r, erecv_r, right).start()
        remote(wbuf.at[0, at], from_r.at[at], esend_l, erecv_l, left).start()

    for e in range(half):
        square(e)
    pl.semaphore_wait(barrier, len(near))
    signal(tok_l.at[0], right)
    signal(tok_r.at[0], left)
    early(pl.ds(0, FIRST))
    for e in range(half, experts):
        square(e)

    mine, theirs = pl.ds(core * half, half), pl.ds((1 - core) * half, half)
    swap = remote(part.at[theirs], other, osem.at[0], osem.at[1], partner)
    swap.start()
    for d in range(2, reach + 1):
        pl.semaphore_wait(tok_l.at[d - 2], 1)
        if d < reach:
            signal(tok_l.at[d - 1], right)
            pl.semaphore_wait(tok_r.at[d - 2], 1)
            if d < reach - 1:
                signal(tok_r.at[d - 1], left)
    swap.wait_recv()
    sums[z] = part[mine] + other[...]
    peers = [{"zero": ((z + j) % chips) * 2 + core} for j in range(1, chips)]
    peers = sorted(zip(range(1, chips), peers), key=lambda p: -min(p[0], chips - p[0]))
    for _, to in peers:
        remote(sums.at[z], sums.at[z], ssem.at[0], ssem.at[1], to).start()
    if ahead > FIRST:
        for g in range(FIRST // lanes, ahead // lanes):
            early(pl.ds(g * lanes, lanes))
    for copy in small:
        copy.wait()
    rblk[core, bank, z] = rw_ref[...] * gain_ref[...]

    most = sums.at[pl.ds(0, chips - 1)]
    full = remote(most, most, ssem.at[0], ssem.at[1], partner)
    full.wait_recv()
    acc = sums[0]
    for k in range(1, chips):
        acc = acc + sums[k]
    total[mine] = acc
    back = remote(total.at[mine], total.at[mine], tsem.at[0], tsem.at[1], partner)
    back.start()
    back.wait_recv()

    def place(k, src):
        return big.at[k // SPLIT, pl.ds((k % SPLIT) * piece, piece),
                      pl.ds(pl.multiple_of(src * lanes, lanes), lanes)]

    def to_right(slot, k, src):
        return remote(place(k, src), place(k, src), send_r, rsem_r.at[slot], right)

    def to_left(slot, k, src):
        return remote(place(k, src), place(k, src), send_l, rsem_l.at[slot], left)

    def to_partner(k, src):
        return remote(place(k, src), place(k, src), send_p, recv_p, partner)

    def serve(k, src, read):
        e, s = k // SPLIT, k % SPLIT
        root = jnp.sqrt(total[e])
        columns = pl.ds(pl.multiple_of(src * lanes, lanes), lanes)
        for g in range(s * groups // SPLIT, (s + 1) * groups // SPLIT):
            at = pl.ds(g * lanes, lanes)
            col = jnp.sum(jnp.where(eye, root[g:g + 1, :], 0.0), axis=1, keepdims=True)
            big[e, at, columns] = (read(e, at) / col).astype(jnp.bfloat16)

    for k in [*range(EARLY, chunks), *range(EARLY)]:
        serve(k, zero, lambda e, at: wbuf[e, at, :])
        if k >= EARLY:
            to_right(k, k, zero).start()
            to_left(k, k, zero).start()
        to_partner(k, zero).start()
    for e in range(experts):
        root = jnp.sqrt(total[e])
        for g in range(groups):
            scale_ref[e:e + 1, g * lanes:(g + 1) * lanes] = root[g:g + 1, :]

    from_left = [{}] + [((z + chips - d) % chips) * 2 + core for d in range(1, reach + 1)]
    from_right = [{}] + [((z + d) % chips) * 2 + core for d in range(1, reach + 1)]

    def on_right(d, slot, k):
        if d < reach - 1:
            to_right(slot + chunks, k, from_left[d]).start()
        elif d == reach - 1 and k % 2 == 0:
            to_right(d * chunks + k // 2, k, from_left[d]).start()
        to_partner(k, from_left[d]).start()

    def on_left(d, slot, k):
        if d < reach - 1:
            to_left(slot + chunks, k, from_right[d]).start()
        elif d == reach - 1 and k % 2 == 1:
            to_left(d * chunks + k // 2, k, from_right[d]).start()
        to_partner(k, from_right[d]).start()

    rows_ahead = wbuf.at[0, pl.ds(0, ahead)]
    remote(rows_ahead, from_l, esend_r, erecv_r, right).wait_recv()
    remote(rows_ahead, from_r, esend_l, erecv_l, left).wait_recv()
    for k in range(EARLY):
        serve(k, from_left[1], lambda e, at: from_l[at, :])
        on_right(1, k, k)
        serve(k, from_right[1], lambda e, at: from_r[at, :])
        on_left(1, k, k)

    def router_z():
        for _, to in peers:
            remote(rblk.at[core, bank, z], rblk.at[core, bank, z], rsend.at[0], rrecv.at[0], to).start()

    def router_wait(n, ref):
        remote(ref, ref, rsend.at[n], rrecv.at[n], partner).wait()

    def router_x():
        router_wait(0, rblk.at[core, bank, pl.ds(0, chips - 1)])
        own = rblk.at[core, bank]
        remote(own, own, rsend.at[1], rrecv.at[1], x_up).start()
        remote(own, own, rsend.at[1], rrecv.at[1], x_down).start()

    def router_x2():
        router_wait(1, rblk.at[core, pl.ds(0, 2)])
        for j in range(2, SIDE - 1):
            own = rblk.at[core, y * SIDE + (x + SIDE + 1 - j) % SIDE]
            remote(own, own, rsend.at[2], rrecv.at[2], x_up).start()

    def router_y():
        router_wait(2, rblk.at[core, 0])
        own = rblk.at[core, pl.ds(y * SIDE, SIDE)]
        remote(own, own, rsend.at[3], rrecv.at[3], y_up).start()
        remote(own, own, rsend.at[3], rrecv.at[3], y_down).start()

    def router_y2():
        router_wait(3, rblk.at[core, pl.ds(0, 2 * SIDE)])
        own = rblk.at[core, pl.ds(((y + tall - 1) % tall) * SIDE, SIDE)]
        remote(own, own, rsend.at[4], rrecv.at[4], y_up).start()

    def router_partner():
        router_wait(4, rblk.at[core, pl.ds(0, SIDE)])
        remote(rblk.at[core], rblk.at[core], rsend.at[5], rrecv.at[5], partner).start()

    def router_finish():
        router_wait(5, rblk.at[core])
        for b in range(banks // 4):
            for q in range(2 * chips):
                block = jnp.concatenate([rblk[q % 2, 4 * b + i, q // 2] for i in range(4)], axis=0)
                n = block.shape[0]
                router_ref[b * n:(b + 1) * n, q * lanes:(q + 1) * lanes] = block.astype(jnp.bfloat16)

    router_steps = [router_x, router_x2, router_y, router_y2, router_partner, router_finish]
    router_z()

    slot = 0
    for d in range(1, reach + 1):
        last = d == reach
        for i in range(chunks // 2 if last else chunks):
            kr = 2 * i if last else i
            kl = 2 * i + 1 if last else i
            if d > 1 or i >= EARLY:
                to_right(slot, kr, from_left[d]).wait_recv()
                on_right(d, slot, kr)
                to_left(slot, kl, from_right[d]).wait_recv()
                on_left(d, slot, kl)
            slot += 1
            if slot % 8 == 0 and router_steps:
                router_steps.pop(0)()

    full.wait_send()
    swap.wait_send()
    back.wait_send()
    remote(rows_ahead, from_l, esend_r, erecv_r, right).wait_send()
    remote(rows_ahead, from_r, esend_l, erecv_l, left).wait_send()
    sent = (chunks * (chips - 1) // 2 - EARLY) * piece // (2 * chips)
    hops = big.at[0, pl.ds(0, sent), :]
    remote(hops, hops, send_r, rsem_r.at[0], right).wait_send()
    remote(hops, hops, send_l, rsem_l.at[0], left).wait_send()
    whole = big.at[:, :, pl.ds(0, chips * lanes)]
    remote(whole, whole, send_p, recv_p, partner).wait()


def out_kernel(big, scale, router, big_hbm, scale_hbm, router_hbm, sems):
    n = big.shape[0]
    copies = [pltpu.make_async_copy(big.at[e], big_hbm.at[e], sems.at[e]) for e in range(n)]
    copies.append(pltpu.make_async_copy(scale, scale_hbm, sems.at[n]))
    copies.append(pltpu.make_async_copy(router, router_hbm, sems.at[n + 1]))
    for copy in copies:
        copy.start()
    for copy in copies:
        copy.wait()


def solution(mesh):
    banks, zeros = mesh.shape["bank"], mesh.shape["zero"]
    chips = zeros // 2

    def shards(w_down, avg_down, router_weight, router_gain):
        experts, rows, lanes = w_down.shape
        width = lanes * zeros
        cols = router_weight.shape[1]
        vmem = pl.BlockSpec(memory_space=pltpu.VMEM)
        hbm = pl.BlockSpec(memory_space=pltpu.HBM)
        pin = lambda x: pltpu.with_memory_space_constraint(x, pltpu.HBM)
        half = experts // 2
        groups = rows // lanes
        slots = experts * SPLIT * (chips - 1) // 2
        ahead = EARLY * rows // SPLIT
        reach = chips // 2
        dma = pltpu.SemaphoreType.DMA
        regular = pltpu.SemaphoreType.REGULAR
        big, scale, router = pl.pallas_call(
            functools.partial(gather_kernel, banks, chips),
            out_shape=(
                jax.ShapeDtypeStruct((experts, rows, width), jnp.bfloat16),
                jax.ShapeDtypeStruct((experts, rows), jnp.float32),
                jax.ShapeDtypeStruct((cols * banks, width), jnp.bfloat16),
            ),
            in_specs=[hbm] * 4,
            out_specs=(vmem, vmem, vmem),
            scratch_shapes=[
                pltpu.VMEM((experts, rows, lanes), jnp.float32),
                pltpu.VMEM((experts, rows, lanes), jnp.bfloat16),
                pltpu.VMEM((cols, lanes), jnp.float32),
                pltpu.VMEM((1, lanes), jnp.float32),
                pltpu.VMEM((experts, groups, lanes), jnp.float32),
                pltpu.VMEM((half, groups, lanes), jnp.float32),
                pltpu.VMEM((chips, half, groups, lanes), jnp.float32),
                pltpu.VMEM((experts, groups, lanes), jnp.float32),
                pltpu.VMEM((2, banks, chips, cols, lanes), jnp.float32),
                pltpu.VMEM((ahead, lanes), jnp.float32),
                pltpu.VMEM((ahead, lanes), jnp.float32),
                dma((experts + 1,)), dma((experts + 1,)), dma((2,)), dma((2,)), dma((2,)),
                regular((reach - 1,)), regular((reach - 2,)),
                dma((slots,)), dma((slots,)), dma(()), dma(()), dma(()), dma(()), dma(()), dma(()),
                dma(()), dma(()), dma((6,)), dma((6,)),
            ],
            compiler_params=pltpu.CompilerParams(
                collective_id=0, has_side_effects=True, vmem_limit_bytes=8 * 1024 * 1024),
            name="gather",
        )(pin(w_down), pin(avg_down), pin(router_weight.T), pin(router_gain.reshape(1, lanes)))
        big, scale, router = pl.pallas_call(
            out_kernel,
            out_shape=(
                jax.ShapeDtypeStruct(big.shape, big.dtype),
                jax.ShapeDtypeStruct(scale.shape, scale.dtype),
                jax.ShapeDtypeStruct(router.shape, router.dtype),
            ),
            in_specs=[vmem, vmem, vmem],
            out_specs=(hbm, hbm, hbm),
            scratch_shapes=[dma((experts + 2,))],
            compiler_params=pltpu.CompilerParams(vmem_limit_bytes=4 * 1024 * 1024),
            name="put_out",
        )(big, scale, router)
        return big, scale, router.T

    return jax.shard_map(
        shards,
        mesh=mesh,
        in_specs=(P("bank", None, "zero"), P("bank", None, "zero"), P("zero", "bank"), P("zero")),
        out_specs=(P("bank", None, None), P("bank", None), P()),
        check_vma=False,
    )
```

time: 107 us -> 106 us (level)
    pallas_call x1, Pallas kernels: 100 us -> 98.9 us  [shards(): pl.pallas_call(functools.partial(gather_kernel, banks, chips), out_shape=...]
where the time goes in v2:
time: 106 us
  Pallas kernels  105 us (99%)
    pallas_call x1, Pallas kernels, shards(): pl.pallas_call(functools.partial(gather_kernel, banks, chips), out_shape=...  98.9 us
    pallas_call x1, Pallas kernels, shards(): pl.pallas_call(out_kernel, out_shape=(jax.ShapeDtypeStruct(big.shape, big...  5.98 us

profile of v2, /device:TPU:1, one launch (start us, length us, event | category | flops | bytes accessed | tf_op | source)
XLA Modules:
  0.0 105.5 jit_solution(17631954883240402536)
XLA Ops:
  0.6 98.9 %gather.1 = (bf16[4,1024,2048]{2,1,0:T(8,128)(2,1)S(1)}, f32[4,1024]{1,0:T(4,128)S(1)}, bf16[64,2048]{1,0:T(8,128)(2,1)S(1)}) custom-call(f32[4,1024,128]{2,1,0:T(8,128)} %w_hbm.1, bf16[4,1024,128]{2,1,0:T(8,128)(2,1)} %avg_hbm.1, f32[4,128]{1,0:T(4,128)} %bitcast.3, f32[1,128]{1,0:T(1,128)} %bitcast.4), custom_call_target="tpu_custom_call" | custom-call | tf_op jit(solution)/shard_map/gather/pallas_call | solution.py:289
  99.6 6.0 %put_out.1 = (bf16[4,1024,2048]{2,1,0:T(8,128)(2,1)}, f32[4,1024]{1,0:T(4,128)}, bf16[64,2048]{1,0:T(8,128)(2,1)}) custom-call(bf16[4,1024,2048]{2,1,0:T(8,128)(2,1)S(1)} %get-tuple-element.9.big, f32[4,1024]{1,0:T(4,128)S(1)} %get-tuple-element.10.scale, bf16[64,2048]{1,0:T(8,128)(2,1)S(1)} %get-tuple-element.11.router), custom_call_target="tpu_custom_call" | custom-call | tf_op jit(solution)/shard_map/put_out/pallas_call | solution.py:319

commit v3 on v2

--- a/solution.py
+++ b/solution.py
@@ -8,9 +8,8 @@
 from jax.sharding import PartitionSpec as P
 
 MESH = pl.DeviceIdType.MESH
-SPLIT = 4
-EARLY = 3
-FIRST = 128
+SPLIT = 2
+EARLY = (2, 0)
 SIDE = 4
 
 
@@ -33,12 +32,11 @@
     partner = {"zero": z * 2 + (1 - core)}
     x_up, x_down = {"bank": y * SIDE + (x + 1) % SIDE}, {"bank": y * SIDE + (x + SIDE - 1) % SIDE}
     y_up, y_down = {"bank": ((y + 1) % tall) * SIDE + x}, {"bank": ((y + tall - 1) % tall) * SIDE + x}
-    half = experts // 2
     groups = rows // lanes
     piece = rows // SPLIT
     chunks = experts * SPLIT
     reach = chips // 2
-    ahead = EARLY * piece
+    early = EARLY[1] + (EARLY[0] - EARLY[1]) * (1 - core)
 
     def remote(src, dst, send, recv, to):
         return pltpu.make_async_remote_copy(src, dst, send, recv, device_id=to, device_id_type=MESH)
@@ -78,22 +76,45 @@
             row = jnp.sum(fresh * fresh, axis=1, keepdims=True)
             part[e, g:g + 1, :] = jnp.sum(jnp.where(eye, row, 0.0), axis=0, keepdims=True)
 
-    def early(at):
-        remote(wbuf.at[0, at], from_l.at[at], esend_r, erecv_r, right).start()
-        remote(wbuf.at[0, at], from_r.at[at], esend_l, erecv_l, left).start()
-
-    for e in range(half):
-        square(e)
+    def ahead(k):
+        return wbuf.at[k // SPLIT, pl.ds(pl.multiple_of(k % SPLIT * piece, piece), piece)]
+
+    def early_right(k):
+        return remote(ahead(k), from_l.at[k], esend_r, erecv_r.at[k], right)
+
+    def early_left(k):
+        return remote(ahead(k), from_r.at[k], esend_l, erecv_l.at[k], left)
+
+    def send_early(k, _):
+        early_right(k).start()
+        early_left(k).start()
+        return 0
+
+    first, second = core == 0, core == 1
+
+    square(0)
     pl.semaphore_wait(barrier, len(near))
     signal(tok_l.at[0], right)
     signal(tok_r.at[0], left)
-    early(pl.ds(0, FIRST))
-    for e in range(half, experts):
-        square(e)
-
-    mine, theirs = pl.ds(core * half, half), pl.ds((1 - core) * half, half)
-    swap = remote(part.at[theirs], other, osem.at[0], osem.at[1], partner)
-    swap.start()
+    for e in range(1, experts + 1):
+        if e * SPLIT - SPLIT < EARLY[0]:
+            @pl.when(first)
+            def _():
+                lax.fori_loop(e * SPLIT - SPLIT, min(e * SPLIT, EARLY[0]), send_early, 0)
+        if e < experts:
+            square(e)
+
+    swap = remote(part, other, osem.at[0], osem.at[1], partner)
+    back = remote(total, total, tsem.at[0], tsem.at[1], partner)
+    peers = [{"zero": ((z + j) % chips) * 2 + core} for j in range(1, chips)]
+    peers = [to for _, to in sorted(zip(range(1, chips), peers), key=lambda p: -min(p[0], chips - p[0]))]
+    most = sums.at[pl.ds(0, chips - 1)]
+    full = remote(most, most, ssem.at[0], ssem.at[1], partner)
+
+    @pl.when(first)
+    def _():
+        swap.start()
+
     for d in range(2, reach + 1):
         pl.semaphore_wait(tok_l.at[d - 2], 1)
         if d < reach:
@@ -101,32 +122,34 @@
             pl.semaphore_wait(tok_r.at[d - 2], 1)
             if d < reach - 1:
                 signal(tok_r.at[d - 1], left)
-    swap.wait_recv()
-    sums[z] = part[mine] + other[...]
-    peers = [{"zero": ((z + j) % chips) * 2 + core} for j in range(1, chips)]
-    peers = sorted(zip(range(1, chips), peers), key=lambda p: -min(p[0], chips - p[0]))
-    for _, to in peers:
-        remote(sums.at[z], sums.at[z], ssem.at[0], ssem.at[1], to).start()
-    if ahead > FIRST:
-        for g in range(FIRST // lanes, ahead // lanes):
-            early(pl.ds(g * lanes, lanes))
+
+    @pl.when(second)
+    def _():
+        swap.wait_recv()
+        sums[z] = part[...] + other[...]
+        for to in peers:
+            remote(sums.at[z], sums.at[z], ssem.at[0], ssem.at[1], to).start()
+        lax.fori_loop(0, EARLY[1], send_early, 0)
+
     for copy in small:
         copy.wait()
     rblk[core, bank, z] = rw_ref[...] * gain_ref[...]
 
-    most = sums.at[pl.ds(0, chips - 1)]
-    full = remote(most, most, ssem.at[0], ssem.at[1], partner)
-    full.wait_recv()
-    acc = sums[0]
-    for k in range(1, chips):
-        acc = acc + sums[k]
-    total[mine] = acc
-    back = remote(total.at[mine], total.at[mine], tsem.at[0], tsem.at[1], partner)
-    back.start()
-    back.wait_recv()
+    @pl.when(second)
+    def _():
+        full.wait_recv()
+        acc = sums[0]
+        for k in range(1, chips):
+            acc = acc + sums[k]
+        total[...] = acc
+        back.start()
+
+    @pl.when(first)
+    def _():
+        back.wait_recv()
 
     def place(k, src):
-        return big.at[k // SPLIT, pl.ds((k % SPLIT) * piece, piece),
+        return big.at[k // SPLIT, pl.ds(pl.multiple_of(k % SPLIT * piece, piece), piece),
                       pl.ds(pl.multiple_of(src * lanes, lanes), lanes)]
 
     def to_right(slot, k, src):
@@ -139,20 +162,34 @@
         return remote(place(k, src), place(k, src), send_p, recv_p, partner)
 
     def serve(k, src, read):
-        e, s = k // SPLIT, k % SPLIT
-        root = jnp.sqrt(total[e])
+        e = k // SPLIT
         columns = pl.ds(pl.multiple_of(src * lanes, lanes), lanes)
-        for g in range(s * groups // SPLIT, (s + 1) * groups // SPLIT):
-            at = pl.ds(g * lanes, lanes)
-            col = jnp.sum(jnp.where(eye, root[g:g + 1, :], 0.0), axis=1, keepdims=True)
-            big[e, at, columns] = (read(e, at) / col).astype(jnp.bfloat16)
-
-    for k in [*range(EARLY, chunks), *range(EARLY)]:
-        serve(k, zero, lambda e, at: wbuf[e, at, :])
-        if k >= EARLY:
-            to_right(k, k, zero).start()
-            to_left(k, k, zero).start()
+        for j in range(groups // SPLIT):
+            g = k % SPLIT * (groups // SPLIT) + j
+            at = pl.ds(pl.multiple_of(g * lanes, lanes), lanes)
+            root = jnp.sqrt(total[e, pl.ds(g, 1), :])
+            col = jnp.sum(jnp.where(eye, root, 0.0), axis=1, keepdims=True)
+            big[e, at, columns] = (read(j) / col).astype(jnp.bfloat16)
+
+    def own(k):
+        def read(j):
+            g = k % SPLIT * (groups // SPLIT) + j
+            return wbuf[k // SPLIT, pl.ds(pl.multiple_of(g * lanes, lanes), lanes), :]
+        serve(k, zero, read)
         to_partner(k, zero).start()
+
+    def own_late(k, _):
+        own(k)
+        to_right(k, k, zero).start()
+        to_left(k, k, zero).start()
+        return 0
+
+    def own_early(k, _):
+        own(k)
+        return 0
+
+    lax.fori_loop(early, chunks, own_late, 0)
+    lax.fori_loop(0, early, own_early, 0)
     for e in range(experts):
         root = jnp.sqrt(total[e])
         for g in range(groups):
@@ -175,17 +212,24 @@
             to_left(d * chunks + k // 2, k, from_right[d]).start()
         to_partner(k, from_right[d]).start()
 
-    rows_ahead = wbuf.at[0, pl.ds(0, ahead)]
-    remote(rows_ahead, from_l, esend_r, erecv_r, right).wait_recv()
-    remote(rows_ahead, from_r, esend_l, erecv_l, left).wait_recv()
-    for k in range(EARLY):
-        serve(k, from_left[1], lambda e, at: from_l[at, :])
+    def convert(k, _):
+        early_right(k).wait_recv()
+        serve(k, from_left[1], lambda j: from_l[k, j * lanes:(j + 1) * lanes, :])
         on_right(1, k, k)
-        serve(k, from_right[1], lambda e, at: from_r[at, :])
+        early_left(k).wait_recv()
+        serve(k, from_right[1], lambda j: from_r[k, j * lanes:(j + 1) * lanes, :])
         on_left(1, k, k)
+        return 0
+
+    def pass_on(k, _):
+        to_right(k, k, from_left[1]).wait_recv()
+        on_right(1, k, k)
+        to_left(k, k, from_right[1]).wait_recv()
+        on_left(1, k, k)
+        return 0
 
     def router_z():
-        for _, to in peers:
+        for to in peers:
             remote(rblk.at[core, bank, z], rblk.at[core, bank, z], rsend.at[0], rrecv.at[0], to).start()
 
     def router_wait(n, ref):
@@ -229,30 +273,39 @@
     router_steps = [router_x, router_x2, router_y, router_y2, router_partner, router_finish]
     router_z()
 
-    slot = 0
-    for d in range(1, reach + 1):
+    lax.fori_loop(0, early, convert, 0)
+    lax.fori_loop(early, chunks, pass_on, 0)
+    router_steps.pop(0)()
+    slot = chunks
+    for d in range(2, reach + 1):
         last = d == reach
         for i in range(chunks // 2 if last else chunks):
             kr = 2 * i if last else i
             kl = 2 * i + 1 if last else i
-            if d > 1 or i >= EARLY:
-                to_right(slot, kr, from_left[d]).wait_recv()
-                on_right(d, slot, kr)
-                to_left(slot, kl, from_right[d]).wait_recv()
-                on_left(d, slot, kl)
+            to_right(slot, kr, from_left[d]).wait_recv()
+            on_right(d, slot, kr)
+            to_left(slot, kl, from_right[d]).wait_recv()
+            on_left(d, slot, kl)
             slot += 1
-            if slot % 8 == 0 and router_steps:
+            if slot % 4 == 2 and router_steps:
                 router_steps.pop(0)()
 
-    full.wait_send()
-    swap.wait_send()
-    back.wait_send()
-    remote(rows_ahead, from_l, esend_r, erecv_r, right).wait_send()
-    remote(rows_ahead, from_r, esend_l, erecv_l, left).wait_send()
-    sent = (chunks * (chips - 1) // 2 - EARLY) * piece // (2 * chips)
-    hops = big.at[0, pl.ds(0, sent), :]
-    remote(hops, hops, send_r, rsem_r.at[0], right).wait_send()
-    remote(hops, hops, send_l, rsem_l.at[0], left).wait_send()
+    for side in range(2):
+        @pl.when(core == side)
+        def _():
+            if side == 0:
+                swap.wait_send()
+            else:
+                full.wait_send()
+                back.wait_send()
+            if EARLY[side] > 0:
+                rows_ahead = from_l.at[pl.ds(0, EARLY[side])]
+                remote(rows_ahead, rows_ahead, esend_r, erecv_r.at[0], right).wait_send()
+                remote(rows_ahead, rows_ahead, esend_l, erecv_l.at[0], left).wait_send()
+            sent = (chunks * (chips - 1) // 2 - EARLY[side]) * piece // (2 * chips)
+            hops = big.at[0, pl.ds(0, sent), :]
+            remote(hops, hops, send_r, rsem_r.at[0], right).wait_send()
+            remote(hops, hops, send_l, rsem_l.at[0], left).wait_send()
     whole = big.at[:, :, pl.ds(0, chips * lanes)]
     remote(whole, whole, send_p, recv_p, partner).wait()
 
@@ -279,10 +332,9 @@
         vmem = pl.BlockSpec(memory_space=pltpu.VMEM)
         hbm = pl.BlockSpec(memory_space=pltpu.HBM)
         pin = lambda x: pltpu.with_memory_space_constraint(x, pltpu.HBM)
-        half = experts // 2
         groups = rows // lanes
         slots = experts * SPLIT * (chips - 1) // 2
-        ahead = EARLY * rows // SPLIT
+        chunk = (max(*EARLY, 1), rows // SPLIT, lanes)
         reach = chips // 2
         dma = pltpu.SemaphoreType.DMA
         regular = pltpu.SemaphoreType.REGULAR
@@ -301,19 +353,19 @@
                 pltpu.VMEM((cols, lanes), jnp.float32),
                 pltpu.VMEM((1, lanes), jnp.float32),
                 pltpu.VMEM((experts, groups, lanes), jnp.float32),
-                pltpu.VMEM((half, groups, lanes), jnp.float32),
-                pltpu.VMEM((chips, half, groups, lanes), jnp.float32),
+                pltpu.VMEM((experts, groups, lanes), jnp.float32),
+                pltpu.VMEM((chips, experts, groups, lanes), jnp.float32),
                 pltpu.VMEM((experts, groups, lanes), jnp.float32),
                 pltpu.VMEM((2, banks, chips, cols, lanes), jnp.float32),
-                pltpu.VMEM((ahead, lanes), jnp.float32),
-                pltpu.VMEM((ahead, lanes), jnp.float32),
+                pltpu.VMEM(chunk, jnp.float32),
+                pltpu.VMEM(chunk, jnp.float32),
                 dma((experts + 1,)), dma((experts + 1,)), dma((2,)), dma((2,)), dma((2,)),
                 regular((reach - 1,)), regular((reach - 2,)),
-                dma((slots,)), dma((slots,)), dma(()), dma(()), dma(()), dma(()), dma(()), dma(()),
+                dma((slots,)), dma((slots,)), dma(()), dma(()), dma(()), dma(()), dma(chunk[:1]), dma(chunk[:1]),
                 dma(()), dma(()), dma((6,)), dma((6,)),
             ],
             compiler_params=pltpu.CompilerParams(
-                collective_id=0, has_side_effects=True, vmem_limit_bytes=8 * 1024 * 1024),
+                collective_id=0, has_side_effects=True, vmem_limit_bytes=12 * 1024 * 1024),
             name="gather",
         )(pin(w_down), pin(avg_down), pin(router_weight.T), pin(router_gain.reshape(1, lanes)))
         big, scale, router = pl.pallas_call(

time: 106 us -> 103 us (0.972)
  Pallas kernels: 105 us -> 103 us
    pallas_call x1, Pallas kernels: 98.9 us -> 96.7 us  [shards(): pl.pallas_call(functools.partial(gather_kernel, banks, chips), out_shape=...]
where the time goes in v3:
time: 103 us
  Pallas kernels  103 us (100%)
    pallas_call x1, Pallas kernels, shards(): pl.pallas_call(functools.partial(gather_kernel, banks, chips), out_shape=...  96.7 us
    pallas_call x1, Pallas kernels, shards(): pl.pallas_call(out_kernel, out_shape=(jax.ShapeDtypeStruct(big.shape, big...  5.98 us

profile of v3, /device:TPU:1, one launch (start us, length us, event | category | flops | bytes accessed | tf_op | source)
XLA Modules:
  0.0 103.3 jit_solution(7739835167635935863)
XLA Ops:
  0.6 96.7 %gather.1 = (bf16[4,1024,2048]{2,1,0:T(8,128)(2,1)S(1)}, f32[4,1024]{1,0:T(4,128)S(1)}, bf16[64,2048]{1,0:T(8,128)(2,1)S(1)}) custom-call(f32[4,1024,128]{2,1,0:T(8,128)} %w_hbm.1, bf16[4,1024,128]{2,1,0:T(8,128)(2,1)} %avg_hbm.1, f32[4,128]{1,0:T(4,128)} %bitcast.3, f32[1,128]{1,0:T(1,128)} %bitcast.4), custom_call_target="tpu_custom_call" | custom-call | tf_op jit(solution)/shard_map/gather/pallas_call | solution.py:341
  97.3 6.0 %put_out.1 = (bf16[4,1024,2048]{2,1,0:T(8,128)(2,1)}, f32[4,1024]{1,0:T(4,128)}, bf16[64,2048]{1,0:T(8,128)(2,1)}) custom-call(bf16[4,1024,2048]{2,1,0:T(8,128)(2,1)S(1)} %get-tuple-element.9.big, f32[4,1024]{1,0:T(4,128)S(1)} %get-tuple-element.10.scale, bf16[64,2048]{1,0:T(8,128)(2,1)S(1)} %get-tuple-element.11.router), custom_call_target="tpu_custom_call" | custom-call | tf_op jit(solution)/shard_map/put_out/pallas_call | solution.py:371

commit v4 on v3

--- a/solution.py
+++ b/solution.py
@@ -11,13 +11,14 @@
 SPLIT = 2
 EARLY = (2, 0)
 SIDE = 4
+PLANE = 1
 
 
 def gather_kernel(
     banks, chips, w_hbm, avg_hbm, rw_hbm, gain_hbm,
     big, scale_ref, router_ref,
     wbuf, abuf, rw_ref, gain_ref, part, other, sums, total, rblk, from_l, from_r,
-    wsem, asem, osem, ssem, tsem, tok_l, tok_r,
+    wsem, asem, osem, ssem, tsem, tok_l, tok_r, tok_x, tok_z,
     rsem_r, rsem_l, send_r, send_l, esend_r, esend_l, erecv_r, erecv_l, send_p, recv_p, rsend, rrecv,
 ):
     experts, rows, lanes = wbuf.shape
@@ -57,9 +58,14 @@
         copy.start()
 
     barrier = pltpu.get_barrier_semaphore()
-    near = (left, right, partner, x_up, x_down, y_up, y_down)
+    near, across = (left, right, partner), (x_up, x_down, y_up, y_down)
     for to in near:
         signal(barrier, to)
+
+    @pl.when(z == PLANE)
+    def _():
+        for to in across:
+            signal(barrier, to)
 
     eye = (
         lax.broadcasted_iota(jnp.int32, (lanes, lanes), 0)
@@ -93,7 +99,14 @@
     first, second = core == 0, core == 1
 
     square(0)
-    pl.semaphore_wait(barrier, len(near))
+    @pl.when(z == PLANE)
+    def _():
+        pl.semaphore_wait(barrier, len(near) + len(across))
+
+    @pl.when(z != PLANE)
+    def _():
+        pl.semaphore_wait(barrier, len(near))
+
     signal(tok_l.at[0], right)
     signal(tok_r.at[0], left)
     for e in range(1, experts + 1):
@@ -131,6 +144,11 @@
             remote(sums.at[z], sums.at[z], ssem.at[0], ssem.at[1], to).start()
         lax.fori_loop(0, EARLY[1], send_early, 0)
 
+    @pl.when(z == PLANE)
+    def _():
+        for to in across:
+            signal(tok_x, to)
+
     for copy in small:
         copy.wait()
     rblk[core, bank, z] = rw_ref[...] * gain_ref[...]
@@ -237,6 +255,17 @@
 
     def router_x():
         router_wait(0, rblk.at[core, bank, pl.ds(0, chips - 1)])
+
+        @pl.when(z == PLANE)
+        def _():
+            pl.semaphore_wait(tok_x, len(across))
+            for to in peers:
+                signal(tok_z, to)
+
+        @pl.when(z != PLANE)
+        def _():
+            pl.semaphore_wait(tok_z, 1)
+
         own = rblk.at[core, bank]
         remote(own, own, rsend.at[1], rrecv.at[1], x_up).start()
         remote(own, own, rsend.at[1], rrecv.at[1], x_down).start()
@@ -360,7 +389,7 @@
                 pltpu.VMEM(chunk, jnp.float32),
                 pltpu.VMEM(chunk, jnp.float32),
                 dma((experts + 1,)), dma((experts + 1,)), dma((2,)), dma((2,)), dma((2,)),
-                regular((reach - 1,)), regular((reach - 2,)),
+                regular((reach - 1,)), regular((reach - 2,)), regular, regular,
                 dma((slots,)), dma((slots,)), dma(()), dma(()), dma(()), dma(()), dma(chunk[:1]), dma(chunk[:1]),
                 dma(()), dma(()), dma((6,)), dma((6,)),
             ],

time: 103 us -> 102 us (level)
  Pallas kernels: 103 us -> 101 us
    pallas_call x1, Pallas kernels: 96.7 us -> 95 us  [shards(): pl.pallas_call(functools.partial(gather_kernel, banks, chips), out_shape=...]
where the time goes in v4:
time: 102 us
  Pallas kernels  101 us (99%)
    pallas_call x1, Pallas kernels, shards(): pl.pallas_call(functools.partial(gather_kernel, banks, chips), out_shape=...  95 us
    pallas_call x1, Pallas kernels, shards(): pl.pallas_call(out_kernel, out_shape=(jax.ShapeDtypeStruct(big.shape, big...  5.98 us

profile of v4, /device:TPU:1, one launch (start us, length us, event | category | flops | bytes accessed | tf_op | source)
XLA Modules:
  0.0 101.6 jit_solution(16729341075539492591)
XLA Ops:
  0.6 95.0 %gather.1 = (bf16[4,1024,2048]{2,1,0:T(8,128)(2,1)S(1)}, f32[4,1024]{1,0:T(4,128)S(1)}, bf16[64,2048]{1,0:T(8,128)(2,1)S(1)}) custom-call(f32[4,1024,128]{2,1,0:T(8,128)} %w_hbm.1, bf16[4,1024,128]{2,1,0:T(8,128)(2,1)} %avg_hbm.1, f32[4,128]{1,0:T(4,128)} %bitcast.3, f32[1,128]{1,0:T(1,128)} %bitcast.4), custom_call_target="tpu_custom_call" | custom-call | tf_op jit(solution)/shard_map/gather/pallas_call | solution.py:370
  95.6 6.0 %put_out.1 = (bf16[4,1024,2048]{2,1,0:T(8,128)(2,1)}, f32[4,1024]{1,0:T(4,128)}, bf16[64,2048]{1,0:T(8,128)(2,1)}) custom-call(bf16[4,1024,2048]{2,1,0:T(8,128)(2,1)S(1)} %get-tuple-element.9.big, f32[4,1024]{1,0:T(4,128)S(1)} %get-tuple-element.10.scale, bf16[64,2048]{1,0:T(8,128)(2,1)S(1)} %get-tuple-element.11.router), custom_call_target="tpu_custom_call" | custom-call | tf_op jit(solution)/shard_map/put_out/pallas_call | solution.py:400

commit v5 on v4

--- a/solution.py
+++ b/solution.py
@@ -9,7 +9,7 @@
 
 MESH = pl.DeviceIdType.MESH
 SPLIT = 2
-EARLY = (2, 0)
+STEP, EARLY = 256, 3
 SIDE = 4
 PLANE = 1
 
@@ -37,7 +37,10 @@
     piece = rows // SPLIT
     chunks = experts * SPLIT
     reach = chips // 2
-    early = EARLY[1] + (EARLY[0] - EARLY[1]) * (1 - core)
+    ahead = EARLY * STEP
+    whole_ones = ahead // piece
+    rest = (ahead - whole_ones * piece) % piece
+    late = chunks - whole_ones - (1 if rest else 0)
 
     def remote(src, dst, send, recv, to):
         return pltpu.make_async_remote_copy(src, dst, send, recv, device_id=to, device_id_type=MESH)
@@ -47,13 +50,14 @@
 
     small = [pltpu.make_async_copy(rw_hbm, rw_ref, asem.at[experts]),
              pltpu.make_async_copy(gain_hbm, gain_ref, wsem.at[experts])]
-    loads = []
-    for e in range(experts):
+    loads = {}
+    order = [experts - 1, *range(experts - 1)]
+    for e in order:
         lw = pltpu.make_async_copy(w_hbm.at[e], wbuf.at[e], wsem.at[e])
         la = pltpu.make_async_copy(avg_hbm.at[e], abuf.at[e], asem.at[e])
         lw.start()
         la.start()
-        loads.append((lw, la))
+        loads[e] = (lw, la)
     for copy in small:
         copy.start()
 
@@ -82,23 +86,21 @@
             row = jnp.sum(fresh * fresh, axis=1, keepdims=True)
             part[e, g:g + 1, :] = jnp.sum(jnp.where(eye, row, 0.0), axis=0, keepdims=True)
 
-    def ahead(k):
-        return wbuf.at[k // SPLIT, pl.ds(pl.multiple_of(k % SPLIT * piece, piece), piece)]
-
-    def early_right(k):
-        return remote(ahead(k), from_l.at[k], esend_r, erecv_r.at[k], right)
-
-    def early_left(k):
-        return remote(ahead(k), from_r.at[k], esend_l, erecv_l.at[k], left)
-
-    def send_early(k, _):
-        early_right(k).start()
-        early_left(k).start()
-        return 0
+    def early_rows(p):
+        at = experts * rows - ahead + p * STEP
+        return at // rows, pl.ds(at % rows, STEP)
+
+    def early_right(p):
+        e, at = early_rows(p)
+        return remote(wbuf.at[e, at], from_l.at[p], esend_r, erecv_r.at[p], right)
+
+    def early_left(p):
+        e, at = early_rows(p)
+        return remote(wbuf.at[e, at], from_r.at[p], esend_l, erecv_l.at[p], left)
 
     first, second = core == 0, core == 1
 
-    square(0)
+    square(order[0])
     @pl.when(z == PLANE)
     def _():
         pl.semaphore_wait(barrier, len(near) + len(across))
@@ -109,20 +111,22 @@
 
     signal(tok_l.at[0], right)
     signal(tok_r.at[0], left)
-    for e in range(1, experts + 1):
-        if e * SPLIT - SPLIT < EARLY[0]:
-            @pl.when(first)
-            def _():
-                lax.fori_loop(e * SPLIT - SPLIT, min(e * SPLIT, EARLY[0]), send_early, 0)
-        if e < experts:
-            square(e)
+
+    @pl.when(first)
+    def _():
+        for p in range(EARLY):
+            early_right(p).start()
+            early_left(p).start()
+    for e in order[1:]:
+        square(e)
 
     swap = remote(part, other, osem.at[0], osem.at[1], partner)
-    back = remote(total, total, tsem.at[0], tsem.at[1], partner)
+    batches = [pl.ds(0, 1), pl.ds(1, experts - 1)]
+    backs = [remote(total.at[at], total.at[at], tsem.at[n, 0], tsem.at[n, 1], partner) for n, at in enumerate(batches)]
     peers = [{"zero": ((z + j) % chips) * 2 + core} for j in range(1, chips)]
     peers = [to for _, to in sorted(zip(range(1, chips), peers), key=lambda p: -min(p[0], chips - p[0]))]
-    most = sums.at[pl.ds(0, chips - 1)]
-    full = remote(most, most, ssem.at[0], ssem.at[1], partner)
+    most = [sums.at[pl.ds(0, chips - 1), at] for at in batches]
+    fulls = [remote(ref, ref, ssem.at[n, 0], ssem.at[n, 1], partner) for n, ref in enumerate(most)]
 
     @pl.when(first)
     def _():
@@ -140,9 +144,9 @@
     def _():
         swap.wait_recv()
         sums[z] = part[...] + other[...]
-        for to in peers:
-            remote(sums.at[z], sums.at[z], ssem.at[0], ssem.at[1], to).start()
-        lax.fori_loop(0, EARLY[1], send_early, 0)
+        for n, at in enumerate(batches):
+            for to in peers:
+                remote(sums.at[z, at], sums.at[z, at], ssem.at[n, 0], ssem.at[n, 1], to).start()
 
     @pl.when(z == PLANE)
     def _():
@@ -153,18 +157,19 @@
         copy.wait()
     rblk[core, bank, z] = rw_ref[...] * gain_ref[...]
 
-    @pl.when(second)
-    def _():
-        full.wait_recv()
-        acc = sums[0]
-        for k in range(1, chips):
-            acc = acc + sums[k]
-        total[...] = acc
-        back.start()
-
-    @pl.when(first)
-    def _():
-        back.wait_recv()
+    def known(n):
+        @pl.when(second)
+        def _():
+            fulls[n].wait_recv()
+            acc = sums[0, batches[n]]
+            for k in range(1, chips):
+                acc = acc + sums[k, batches[n]]
+            total[batches[n]] = acc
+            backs[n].start()
+
+        @pl.when(first)
+        def _():
+            backs[n].wait_recv()
 
     def place(k, src):
         return big.at[k // SPLIT, pl.ds(pl.multiple_of(k % SPLIT * piece, piece), piece),
@@ -178,6 +183,23 @@
 
     def to_partner(k, src):
         return remote(place(k, src), place(k, src), send_p, recv_p, partner)
+
+    def part_right(k, src):
+        ref = place(k, src).at[pl.ds(0, piece - rest)]
+        return remote(ref, ref, send_r, rsem_r.at[k], right)
+
+    def part_left(k, src):
+        ref = place(k, src).at[pl.ds(0, piece - rest)]
+        return remote(ref, ref, send_l, rsem_l.at[k], left)
+
+    def serve_early(src, held, p):
+        e, at = early_rows(p)
+        columns = pl.ds(pl.multiple_of(src * lanes, lanes), lanes)
+        for j in range(STEP // lanes):
+            g = at.start // lanes + j
+            root = jnp.sqrt(total[e, g:g + 1, :])
+            col = jnp.sum(jnp.where(eye, root, 0.0), axis=1, keepdims=True)
+            big[e, g * lanes:(g + 1) * lanes, columns] = (held[p, j * lanes:(j + 1) * lanes, :] / col).astype(jnp.bfloat16)
 
     def serve(k, src, read):
         e = k // SPLIT
@@ -202,12 +224,23 @@
         to_left(k, k, zero).start()
         return 0
 
-    def own_early(k, _):
-        own(k)
-        return 0
-
-    lax.fori_loop(early, chunks, own_late, 0)
-    lax.fori_loop(0, early, own_early, 0)
+    known(0)
+    lax.fori_loop(0, SPLIT, own_late, 0)
+    known(1)
+    lax.fori_loop(SPLIT, late, own_late, 0)
+
+    @pl.when(second)
+    def _():
+        lax.fori_loop(late, chunks, own_late, 0)
+
+    @pl.when(first)
+    def _():
+        for k in range(late, chunks):
+            own(k)
+            if rest and k == late:
+                part_right(k, zero).start()
+                part_left(k, zero).start()
+
     for e in range(experts):
         root = jnp.sqrt(total[e])
         for g in range(groups):
@@ -229,15 +262,6 @@
         elif d == reach - 1 and k % 2 == 1:
             to_left(d * chunks + k // 2, k, from_right[d]).start()
         to_partner(k, from_right[d]).start()
-
-    def convert(k, _):
-        early_right(k).wait_recv()
-        serve(k, from_left[1], lambda j: from_l[k, j * lanes:(j + 1) * lanes, :])
-        on_right(1, k, k)
-        early_left(k).wait_recv()
-        serve(k, from_right[1], lambda j: from_r[k, j * lanes:(j + 1) * lanes, :])
-        on_left(1, k, k)
-        return 0
 
     def pass_on(k, _):
         to_right(k, k, from_left[1]).wait_recv()
@@ -302,8 +326,31 @@
     router_steps = [router_x, router_x2, router_y, router_y2, router_partner, router_finish]
     router_z()
 
-    lax.fori_loop(0, early, convert, 0)
-    lax.fori_loop(early, chunks, pass_on, 0)
+    @pl.when(first)
+    def _():
+        for p in range(EARLY):
+            early_right(p).wait_recv()
+            serve_early(from_left[1], from_l, p)
+            early_left(p).wait_recv()
+            serve_early(from_right[1], from_r, p)
+        for k in range(chunks - whole_ones, chunks):
+            on_right(1, k, k)
+            on_left(1, k, k)
+
+    lax.fori_loop(0, late, pass_on, 0)
+
+    @pl.when(second)
+    def _():
+        lax.fori_loop(late, chunks, pass_on, 0)
+
+    if rest:
+        @pl.when(first)
+        def _():
+            part_right(late, from_left[1]).wait_recv()
+            on_right(1, late, late)
+            part_left(late, from_right[1]).wait_recv()
+            on_left(1, late, late)
+
     router_steps.pop(0)()
     slot = chunks
     for d in range(2, reach + 1):
@@ -325,13 +372,12 @@
             if side == 0:
                 swap.wait_send()
             else:
-                full.wait_send()
-                back.wait_send()
-            if EARLY[side] > 0:
-                rows_ahead = from_l.at[pl.ds(0, EARLY[side])]
-                remote(rows_ahead, rows_ahead, esend_r, erecv_r.at[0], right).wait_send()
-                remote(rows_ahead, rows_ahead, esend_l, erecv_l.at[0], left).wait_send()
-            sent = (chunks * (chips - 1) // 2 - EARLY[side]) * piece // (2 * chips)
+                for copy in (*fulls, *backs):
+                    copy.wait_send()
+            if side == 0:
+                remote(from_l, from_l, esend_r, erecv_r.at[0], right).wait_send()
+                remote(from_l, from_l, esend_l, erecv_l.at[0], left).wait_send()
+            sent = (chunks * (chips - 1) // 2 * piece - ahead * (1 - side)) // (2 * chips)
             hops = big.at[0, pl.ds(0, sent), :]
             remote(hops, hops, send_r, rsem_r.at[0], right).wait_send()
             remote(hops, hops, send_l, rsem_l.at[0], left).wait_send()
@@ -363,7 +409,7 @@
         pin = lambda x: pltpu.with_memory_space_constraint(x, pltpu.HBM)
         groups = rows // lanes
         slots = experts * SPLIT * (chips - 1) // 2
-        chunk = (max(*EARLY, 1), rows // SPLIT, lanes)
+        chunk = (EARLY, STEP, lanes)
         reach = chips // 2
         dma = pltpu.SemaphoreType.DMA
         regular = pltpu.SemaphoreType.REGULAR
@@ -388,7 +434,7 @@
                 pltpu.VMEM((2, banks, chips, cols, lanes), jnp.float32),
                 pltpu.VMEM(chunk, jnp.float32),
                 pltpu.VMEM(chunk, jnp.float32),
-                dma((experts + 1,)), dma((experts + 1,)), dma((2,)), dma((2,)), dma((2,)),
+                dma((experts + 1,)), dma((experts + 1,)), dma((2,)), dma((2, 2)), dma((2, 2)),
                 regular((reach - 1,)), regular((reach - 2,)), regular, regular,
                 dma((slots,)), dma((slots,)), dma(()), dma(()), dma(()), dma(()), dma(chunk[:1]), dma(chunk[:1]),
                 dma(()), dma(()), dma((6,)), dma((6,)),

time: 102 us -> 101 us (level)
  no operation moved by 1% of the time
where the time goes in v5:
time: 101 us
  Pallas kernels  101 us (100%)
    pallas_call x1, Pallas kernels, shards(): pl.pallas_call(functools.partial(gather_kernel, banks, chips), out_shape=...  94.5 us
    pallas_call x1, Pallas kernels, shards(): pl.pallas_call(out_kernel, out_shape=(jax.ShapeDtypeStruct(big.shape, big...  5.98 us

profile of v5, /device:TPU:1, one launch (start us, length us, event | category | flops | bytes accessed | tf_op | source)
XLA Modules:
  0.0 101.1 jit_solution(9774246184424433510)
XLA Ops:
  0.6 94.5 %gather.1 = (bf16[4,1024,2048]{2,1,0:T(8,128)(2,1)S(1)}, f32[4,1024]{1,0:T(4,128)S(1)}, bf16[64,2048]{1,0:T(8,128)(2,1)S(1)}) custom-call(f32[4,1024,128]{2,1,0:T(8,128)} %w_hbm.1, bf16[4,1024,128]{2,1,0:T(8,128)(2,1)} %avg_hbm.1, f32[4,128]{1,0:T(4,128)} %bitcast.3, f32[1,128]{1,0:T(1,128)} %bitcast.4), custom_call_target="tpu_custom_call" | custom-call | tf_op jit(solution)/shard_map/gather/pallas_call | solution.py:416
  95.2 6.0 %put_out.1 = (bf16[4,1024,2048]{2,1,0:T(8,128)(2,1)}, f32[4,1024]{1,0:T(4,128)}, bf16[64,2048]{1,0:T(8,128)(2,1)}) custom-call(bf16[4,1024,2048]{2,1,0:T(8,128)(2,1)S(1)} %get-tuple-element.9.big, f32[4,1024]{1,0:T(4,128)S(1)} %get-tuple-element.10.scale, bf16[64,2048]{1,0:T(8,128)(2,1)S(1)} %get-tuple-element.11.router), custom_call_target="tpu_custom_call" | custom-call | tf_op jit(solution)/shard_map/put_out/pallas_call | solution.py:446

commit v6 on v5

--- a/solution.py
+++ b/solution.py
@@ -11,7 +11,7 @@
 SPLIT = 2
 STEP, EARLY = 256, 3
 SIDE = 4
-PLANE = 1
+PLANE = 2
 
 
 def gather_kernel(
@@ -48,6 +48,16 @@
     def signal(sem, to):
         pl.semaphore_signal(sem, inc=1, device_id=to, device_id_type=MESH)
 
+    barrier = pltpu.get_barrier_semaphore()
+    near, across = (left, right, partner), (x_up, x_down, y_up, y_down)
+    for to in near:
+        signal(barrier, to)
+
+    @pl.when(z == PLANE)
+    def _():
+        for to in across:
+            signal(barrier, to)
+
     small = [pltpu.make_async_copy(rw_hbm, rw_ref, asem.at[experts]),
              pltpu.make_async_copy(gain_hbm, gain_ref, wsem.at[experts])]
     loads = {}
@@ -60,16 +70,6 @@
         loads[e] = (lw, la)
     for copy in small:
         copy.start()
-
-    barrier = pltpu.get_barrier_semaphore()
-    near, across = (left, right, partner), (x_up, x_down, y_up, y_down)
-    for to in near:
-        signal(barrier, to)
-
-    @pl.when(z == PLANE)
-    def _():
-        for to in across:
-            signal(barrier, to)
 
     eye = (
         lax.broadcasted_iota(jnp.int32, (lanes, lanes), 0)

time: 101 us -> 101 us (level)
  no operation moved by 1% of the time
where the time goes in v6:
time: 101 us
  Pallas kernels  100 us (99%)
    pallas_call x1, Pallas kernels, shards(): pl.pallas_call(functools.partial(gather_kernel, banks, chips), out_shape=...  94.5 us
    pallas_call x1, Pallas kernels, shards(): pl.pallas_call(out_kernel, out_shape=(jax.ShapeDtypeStruct(big.shape, big...  5.98 us

profile of v6, /device:TPU:1, one launch (start us, length us, event | category | flops | bytes accessed | tf_op | source)
XLA Modules:
  0.0 101.1 jit_solution(9829718237961819230)
XLA Ops:
  0.6 94.5 %gather.1 = (bf16[4,1024,2048]{2,1,0:T(8,128)(2,1)S(1)}, f32[4,1024]{1,0:T(4,128)S(1)}, bf16[64,2048]{1,0:T(8,128)(2,1)S(1)}) custom-call(f32[4,1024,128]{2,1,0:T(8,128)} %w_hbm.1, bf16[4,1024,128]{2,1,0:T(8,128)(2,1)} %avg_hbm.1, f32[4,128]{1,0:T(4,128)} %bitcast.3, f32[1,128]{1,0:T(1,128)} %bitcast.4), custom_call_target="tpu_custom_call" | custom-call | tf_op jit(solution)/shard_map/gather/pallas_call | solution.py:416
  95.1 6.0 %put_out.1 = (bf16[4,1024,2048]{2,1,0:T(8,128)(2,1)}, f32[4,1024]{1,0:T(4,128)}, bf16[64,2048]{1,0:T(8,128)(2,1)}) custom-call(bf16[4,1024,2048]{2,1,0:T(8,128)(2,1)S(1)} %get-tuple-element.9.big, f32[4,1024]{1,0:T(4,128)S(1)} %get-tuple-element.10.scale, bf16[64,2048]{1,0:T(8,128)(2,1)S(1)} %get-tuple-element.11.router), custom_call_target="tpu_custom_call" | custom-call | tf_op jit(solution)/shard_map/put_out/pallas_call | solution.py:446

commit v7 on v5

--- a/solution.py
+++ b/solution.py
@@ -11,7 +11,7 @@
 SPLIT = 2
 STEP, EARLY = 256, 3
 SIDE = 4
-PLANE = 1
+PLANE = 2
 
 
 def gather_kernel(

time: 101 us -> 101 us (level)
  no operation moved by 1% of the time
where the time goes in v7:
time: 101 us
  Pallas kernels  100 us (99%)
    pallas_call x1, Pallas kernels, shards(): pl.pallas_call(functools.partial(gather_kernel, banks, chips), out_shape=...  94.5 us
    pallas_call x1, Pallas kernels, shards(): pl.pallas_call(out_kernel, out_shape=(jax.ShapeDtypeStruct(big.shape, big...  5.98 us

profile of v7, /device:TPU:1, one launch (start us, length us, event | category | flops | bytes accessed | tf_op | source)
XLA Modules:
  0.0 101.1 jit_solution(3617409422820107462)
XLA Ops:
  0.6 94.5 %gather.1 = (bf16[4,1024,2048]{2,1,0:T(8,128)(2,1)S(1)}, f32[4,1024]{1,0:T(4,128)S(1)}, bf16[64,2048]{1,0:T(8,128)(2,1)S(1)}) custom-call(f32[4,1024,128]{2,1,0:T(8,128)} %w_hbm.1, bf16[4,1024,128]{2,1,0:T(8,128)(2,1)} %avg_hbm.1, f32[4,128]{1,0:T(4,128)} %bitcast.3, f32[1,128]{1,0:T(1,128)} %bitcast.4), custom_call_target="tpu_custom_call" | custom-call | tf_op jit(solution)/shard_map/gather/pallas_call | solution.py:416
  95.1 6.0 %put_out.1 = (bf16[4,1024,2048]{2,1,0:T(8,128)(2,1)}, f32[4,1024]{1,0:T(4,128)}, bf16[64,2048]{1,0:T(8,128)(2,1)}) custom-call(bf16[4,1024,2048]{2,1,0:T(8,128)(2,1)S(1)} %get-tuple-element.9.big, f32[4,1024]{1,0:T(4,128)S(1)} %get-tuple-element.10.scale, bf16[64,2048]{1,0:T(8,128)(2,1)S(1)} %get-tuple-element.11.router), custom_call_target="tpu_custom_call" | custom-call | tf_op jit(solution)/shard_map/put_out/pallas_call | solution.py:446
